TPU v7x, 32 devices: a 4x4x1 block of a 4x4x8 slice. The times are simulated.
32 devices in a mesh: data: 1 (over z), expert: 32 (over y, x, core).
Axes of the slice: x: 4, y: 4, z: 1, core: 2. Of those that a mesh axis runs over, the one named last changes fastest.
The devices are a block of a 4x4x8 slice.
Arguments:
- x_a: bfloat16 [32768, 768], P(('data', 'expert'))
- idx_a: int32 [32768, 1], P(('data', 'expert'))
- gate_a: float32 [32768, 1], P(('data', 'expert'))
- x_b: bfloat16 [32768, 768], P(('data', 'expert'))
- idx_b: int32 [32768, 1], P(('data', 'expert'))
- gate_b: float32 [32768, 1], P(('data', 'expert'))
- w_up: bfloat16 [128, 768, 3072], P('expert')
- w_down: bfloat16 [128, 3072, 768], P('expert')
Outputs:
- output 1: bfloat16 [32768, 768], P(('data', 'expert'))
- output 2: bfloat16 [32768, 768], P(('data', 'expert'))
All inputs are finite; a program needn't handle non-finite values.
Results may differ from a plain program's by a relative error of at most 0.001.
Values are sent between devices in bfloat16 or wider.
A program may use at most 768 MiB of HBM per device.

v0:
```python
import jax
import jax.numpy as jnp
from jax import lax
from jax.sharding import PartitionSpec as P


def count_and_rank(flat_ids, n_experts):
    one_hot = (flat_ids[:, None] == jnp.arange(n_experts, dtype=jnp.int32)[None, :]).astype(jnp.int32)
    counts = jnp.sum(one_hot, axis=0)
    local_rank = jnp.sum((jnp.cumsum(one_hot, axis=0) - one_hot) * one_hot, axis=1)
    return counts, local_rank


def slot_plan(all_counts, capacity):
    inclusive = jnp.cumsum(all_counts, axis=0)
    first_slot = jnp.minimum(inclusive - all_counts, capacity)
    kept_count = jnp.minimum(inclusive, capacity) - first_slot
    return first_slot, kept_count


def owner_cols(dev_table, my_index, group_size):
    local_experts = dev_table.shape[1] // group_size
    return jnp.take(dev_table.reshape(group_size, group_size, local_experts), my_index, axis=1)


def dispatch_rows(tok_rows, flat_ids, local_rank, kept_own, max_load):
    n_tokens = tok_rows.shape[0]
    n_experts = kept_own.shape[0]
    n_pairs = flat_ids.shape[0]
    keep_pair = local_rank < jnp.take(kept_own, flat_ids)
    send_pos = jnp.where(keep_pair, flat_ids * max_load + local_rank, n_experts * max_load)
    pair_token = jnp.arange(n_pairs, dtype=jnp.int32) // (n_pairs // n_tokens)
    slot_token = jnp.full((n_experts * max_load,), n_tokens, jnp.int32).at[send_pos].set(pair_token, mode='drop')
    send_rows = jnp.take(tok_rows, slot_token, axis=0, mode='fill', fill_value=0)
    return send_pos, send_rows


def compact_rows(recv_rows, first_mine, kept_mine, capacity, max_load):
    group_size, local_experts = first_mine.shape
    slot_ids = jnp.arange(capacity, dtype=jnp.int32)
    end_mine = first_mine + kept_mine
    source_dev = jnp.sum((end_mine[:, :, None] <= slot_ids[None, None, :]).astype(jnp.int32), axis=0)
    source_safe = jnp.minimum(source_dev, group_size - 1)
    source_first = jnp.take_along_axis(first_mine.T, source_safe, axis=1)
    expert_ids = jnp.arange(local_experts, dtype=jnp.int32)[:, None]
    row_index = (source_safe * local_experts + expert_ids) * max_load + slot_ids[None, :] - source_first
    row_index = jnp.where(source_dev < group_size, row_index, group_size * local_experts * max_load)
    picked = jnp.take(recv_rows, row_index.reshape(-1), axis=0, mode='fill', fill_value=0)
    return picked.reshape(local_experts, capacity, recv_rows.shape[1])


def expert_ffn(expert_in, w_up, w_down):
    hidden = jax.nn.gelu(jnp.einsum('ecd,edf->ecf', expert_in, w_up, preferred_element_type=jnp.float32)).astype(jnp.bfloat16)
    return jnp.einsum('ecf,efd->ecd', hidden, w_down, preferred_element_type=jnp.float32).astype(jnp.bfloat16)


def expand_rows(expert_out, first_mine, kept_mine, max_load):
    local_experts, capacity, model_dim = expert_out.shape
    load_ids = jnp.arange(max_load, dtype=jnp.int32)[None, None, :]
    expert_ids = jnp.arange(local_experts, dtype=jnp.int32)[None, :, None]
    src_index = expert_ids * capacity + first_mine[:, :, None] + load_ids
    src_index = jnp.where(load_ids < kept_mine[:, :, None], src_index, local_experts * capacity)
    return jnp.take(expert_out.reshape(local_experts * capacity, model_dim), src_index.reshape(-1), axis=0, mode='fill', fill_value=0)


def combine_rows(tok_rows, returned, send_pos, gate_vals):
    n_tokens, top_k = gate_vals.shape
    pair_out = jnp.take(returned, send_pos, axis=0, mode='fill', fill_value=0).reshape(n_tokens, top_k, tok_rows.shape[1])
    mix_sum = jnp.einsum('tj,tjd->td', gate_vals, pair_out, preferred_element_type=jnp.float32)
    return (tok_rows.astype(jnp.float32) + mix_sum).astype(jnp.bfloat16)


def moe_micro(tok_rows, route_ids, gate_vals, w_up, w_down, group_size):
    n_tokens, top_k = route_ids.shape
    local_experts = w_up.shape[0]
    n_experts = local_experts * group_size
    n_pairs = n_tokens * top_k
    capacity = n_pairs // local_experts
    max_load = 2 * n_pairs // n_experts
    my_index = lax.axis_index('expert')
    flat_ids = route_ids.reshape(n_pairs)
    counts, local_rank = count_and_rank(flat_ids, n_experts)
    all_counts = lax.all_gather(counts, 'expert')
    first_slot, kept_count = slot_plan(all_counts, capacity)
    send_pos, send_rows = dispatch_rows(tok_rows, flat_ids, local_rank, kept_count[my_index], max_load)
    recv_rows = lax.all_to_all(send_rows, 'expert', 0, 0, tiled=True)
    first_mine = owner_cols(first_slot, my_index, group_size)
    kept_mine = owner_cols(kept_count, my_index, group_size)
    expert_in = compact_rows(recv_rows, first_mine, kept_mine, capacity, max_load)
    expert_out = expert_ffn(expert_in, w_up, w_down)
    back_rows = expand_rows(expert_out, first_mine, kept_mine, max_load)
    returned = lax.all_to_all(back_rows, 'expert', 0, 0, tiled=True)
    return combine_rows(tok_rows, returned, send_pos, gate_vals)


def solution(mesh):
    group_size = mesh.shape['expert']
    row_spec = P(('data', 'expert'), None)
    weight_spec = P('expert', None, None)

    def device_fn(x_a, idx_a, gate_a, x_b, idx_b, gate_b, w_up, w_down):
        y_a = moe_micro(x_a, idx_a, gate_a, w_up, w_down, group_size)
        y_b = moe_micro(x_b, idx_b, gate_b, w_up, w_down, group_size)
        return y_a, y_b

    return jax.shard_map(device_fn, mesh=mesh, in_specs=(row_spec, row_spec, row_spec, row_spec, row_spec, row_spec, weight_spec, weight_spec), out_specs=(row_spec, row_spec), check_vma=False)
```

profile of v0, /device:TPU:98, one launch (start us, length us, event | category | flops | bytes accessed | tf_op | source)
XLA Modules:
  0.0 302.1 jit_solution(1143209295828857824)
XLA Ops:
  3.6 35.3 %all-gather.2 = s32[32,1,128]{2,1,0:T(1,128)S(1)} all-gather(s32[1,1,128]{2,1,0:T(1,128)S(1)} %bitcast.124), channel_id=2, replica_groups=mesh['data'=1,'expert'=32] {'expert'}, dimensions={0}, use_global_device_ids=true | all-gather | bytes 16896 | tf_op jit(solution)/shard_map/all_gather | solution.py:83
  39.8 32.2 %all-gather.3 = s32[32,1,128]{2,1,0:T(1,128)S(1)} all-gather(s32[1,1,128]{2,1,0:T(1,128)S(1)} %bitcast.125), channel_id=3, replica_groups=mesh['data'=1,'expert'=32] {'expert'}, dimensions={0}, use_global_device_ids=true | all-gather | bytes 16896 | tf_op jit(solution)/shard_map/all_gather | solution.py:83
  72.1 6.6 %gather_fusion = s32[1024]{0:T(1024)S(1)} fusion(s32[128]{0:T(128)S(1)} %get-tuple-element.38, s32[1024]{0:T(1024)S(1)} %fusion.59), kind=kCustom, calls=%fused_computation.clone | custom fusion | bytes 12288 | tf_op jit(solution)/shard_map/jit(_take)/gather | solution.py:30
  79.9 4.3 %scatter_custom_fusion = s32[2048]{0:T(1024)S(1)} fusion(s32[1024]{0:T(1024)S(1)} %get-tuple-element.25, s32[1024]{0:T(1024)S(1)} %iota.48, s32[]{:T(128)} %constant.56.clone.1), kind=kCustom, calls=%fused_computation.116 | custom fusion | bytes 8196 | tf_op jit(solution)/shard_map/scatter | solution.py:33
  84.3 9.4 %gather_fusion.1 = bf16[2048,768]{1,0:T(8,128)(2,1)} fusion(bf16[1024,768]{1,0:T(8,128)(2,1)S(1)} %copy-done, s32[2048]{0:T(1024)S(1)} %fusion.44), kind=kCustom, calls=%fused_computation.1.clone | custom fusion | bytes 6299648 | tf_op jit(solution)/shard_map/jit(_take)/gather | solution.py:34
  93.7 3.3 %broadcast_select_fusion.3 = bf16[2048,768]{1,0:T(8,128)(2,1)} fusion(bf16[2048,768]{1,0:T(8,128)(2,1)} %gather_fusion.1, pred[2048]{0:T(1024)(128)(4,1)S(1)} %compare_and_fusion.3), kind=kLoop, calls=%fused_computation.47 | loop fusion | flops 1572864 | bytes 6293504 | tf_op jit(solution)/shard_map/jit(_take)/select_n | solution.py:34
  97.0 5.3 %all-to-all-start = ((bf16[32,64,768]{2,1,0:T(8,128)(2,1)}), bf16[32,64,768]{2,1,0:T(8,128)(2,1)}, u32[]{:S(2)}, u32[]{:S(2)}) async-start(bf16[32,64,768]{2,1,0:T(8,128)(2,1)} %bitcast.14), calls=%async_computation | async-start | bytes 6291456 | tf_op jit(solution)/shard_map/all_to_all | solution.py:86
  103.0 9.0 %gather_fusion.2 = s32[1024]{0:T(1024)S(1)} fusion(s32[4,32]{1,0:T(4,128)S(1)} %get-tuple-element.40, s32[1024]{0:T(1024)S(1)} %bitcast.94), kind=kCustom, calls=%fused_computation.2.clone | custom fusion | bytes 16384 | tf_op jit(solution)/shard_map/jit(take_along_axis)/gather | solution.py:44
  112.5 9.0 %gather_fusion.8 = s32[1024]{0:T(1024)S(1)} fusion(s32[4,32]{1,0:T(4,128)S(1)} %get-tuple-element.41, s32[1024]{0:T(1024)S(1)} %bitcast.93), kind=kCustom, calls=%fused_computation.8.clone | custom fusion | bytes 16384 | tf_op jit(solution)/shard_map/jit(take_along_axis)/gather | solution.py:44
  122.0 6.6 %gather_fusion.6 = s32[1024]{0:T(1024)S(1)} fusion(s32[128]{0:T(128)S(1)} %get-tuple-element.39, s32[1024]{0:T(1024)S(1)} %fusion.58), kind=kCustom, calls=%fused_computation.4.clone | custom fusion | bytes 12288 | tf_op jit(solution)/shard_map/jit(_take)/gather | solution.py:30
  129.2 4.3 %scatter_custom_fusion.1 = s32[2048]{0:T(1024)S(1)} fusion(s32[1024]{0:T(1024)S(1)} %get-tuple-element.23, s32[1024]{0:T(1024)S(1)} %iota.50, s32[]{:T(128)} %constant.56.clone.1), kind=kCustom, calls=%fused_computation.114 | custom fusion | bytes 8196 | tf_op jit(solution)/shard_map/scatter | solution.py:33
  133.6 9.5 %gather_fusion.7 = bf16[2048,768]{1,0:T(8,128)(2,1)} fusion(bf16[1024,768]{1,0:T(8,128)(2,1)S(1)} %copy-done.2, s32[2048]{0:T(1024)S(1)} %fusion.46), kind=kCustom, calls=%fused_computation.6.clone | custom fusion | bytes 6299648 | tf_op jit(solution)/shard_map/jit(_take)/gather | solution.py:34
  144.3 3.3 %broadcast_select_fusion.1 = bf16[2048,768]{1,0:T(8,128)(2,1)} fusion(bf16[2048,768]{1,0:T(8,128)(2,1)} %gather_fusion.7, pred[2048]{0:T(1024)(128)(4,1)S(1)} %compare_and_fusion.1), kind=kLoop, calls=%fused_computation.45 | loop fusion | flops 1572864 | bytes 6293504 | tf_op jit(solution)/shard_map/jit(_take)/select_n | solution.py:34
  147.6 6.7 %all-to-all-start.2 = ((bf16[32,64,768]{2,1,0:T(8,128)(2,1)}), bf16[32,64,768]{2,1,0:T(8,128)(2,1)}, u32[]{:S(2)}, u32[]{:S(2)}) async-start(bf16[32,64,768]{2,1,0:T(8,128)(2,1)} %bitcast.35), calls=%async_computation.2 | async-start | bytes 6291456 | tf_op jit(solution)/shard_map/all_to_all | solution.py:86
  154.4 6.8 %gather_fusion.3 = bf16[1024,768]{1,0:T(8,128)(2,1)S(1)} fusion(bf16[2048,768]{1,0:T(8,128)(2,1)} %bitcast.15, s32[1024]{0:T(1024)S(1)} %fusion.60), kind=kCustom, calls=%fused_computation.3.clone | custom fusion | bytes 3149824 | tf_op jit(solution)/shard_map/jit(_take)/gather | solution.py:48
  161.4 17.2 %fusion.28 = bf16[4,256,768]{2,1,0:T(8,128)(2,1)S(1)} fusion(bf16[4,3072,768]{2,1,0:T(8,128)(2,1)} %param.25, bf16[4,256,768]{2,1,0:T(8,128)(2,1)S(1)} %bitcast.96, bf16[4,768,3072]{2,1,0:T(8,128)(2,1)} %param.24), kind=kOutput, calls=%fused_computation.48 | convolution fusion | flops 9692774400 | bytes 40894464 | tf_op jit(solution)/shard_map/ecf,efd->ecd/dot_general | solution.py:54
  178.5 9.4 %gather_fusion.4 = bf16[2048,768]{1,0:T(8,128)(2,1)} fusion(bf16[1024,768]{1,0:T(8,128)(2,1)S(1)} %bitcast.90, s32[2048]{0:T(1024)S(1)} %fusion.45), kind=kCustom, calls=%fused_computation.5.clone | custom fusion | bytes 6299648 | tf_op jit(solution)/shard_map/jit(_take)/gather | solution.py:63
  188.0 3.2 %broadcast_select_fusion.2 = bf16[2048,768]{1,0:T(8,128)(2,1)} fusion(bf16[2048,768]{1,0:T(8,128)(2,1)} %gather_fusion.4, pred[2048]{0:T(1024)(128)(4,1)S(1)} %compare_and_fusion.2), kind=kLoop, calls=%fused_computation.46 | loop fusion | flops 1572864 | bytes 6293504 | tf_op jit(solution)/shard_map/jit(_take)/select_n | solution.py:63
  191.2 5.2 %all-to-all-done.2 = bf16[32,64,768]{2,1,0:T(8,128)(2,1)} async-done(((bf16[32,64,768]{2,1,0:T(8,128)(2,1)}), bf16[32,64,768]{2,1,0:T(8,128)(2,1)}, u32[]{:S(2)}, u32[]{:S(2)}) %all-to-all-start.2) | async-done | bytes 3145760 | tf_op jit(solution)/shard_map/all_to_all | solution.py:86
  196.4 3.9 %all-to-all-start.1 = ((bf16[32,64,768]{2,1,0:T(8,128)(2,1)}), bf16[32,64,768]{2,1,0:T(8,128)(2,1)}, u32[]{:S(2)}, u32[]{:S(2)}) async-start(bf16[32,64,768]{2,1,0:T(8,128)(2,1)} %bitcast.18), calls=%async_computation.1 | async-start | bytes 6291456 | tf_op jit(solution)/shard_map/all_to_all | solution.py:92
  200.3 6.8 %gather_fusion.9 = bf16[1024,768]{1,0:T(8,128)(2,1)S(1)} fusion(bf16[2048,768]{1,0:T(8,128)(2,1)} %bitcast.36, s32[1024]{0:T(1024)S(1)} %fusion.61), kind=kCustom, calls=%fused_computation.10.clone | custom fusion | bytes 3149824 | tf_op jit(solution)/shard_map/jit(_take)/gather | solution.py:48
  207.3 17.2 %fusion.31 = bf16[4,256,768]{2,1,0:T(8,128)(2,1)S(1)} fusion(bf16[4,3072,768]{2,1,0:T(8,128)(2,1)} %param.25, bf16[4,256,768]{2,1,0:T(8,128)(2,1)S(1)} %bitcast.97, bf16[4,768,3072]{2,1,0:T(8,128)(2,1)} %param.24), kind=kOutput, calls=%fused_computation.49 | convolution fusion | flops 9692774400 | bytes 40894464 | tf_op jit(solution)/shard_map/ecf,efd->ecd/dot_general | solution.py:54
  224.6 9.4 %gather_fusion.10 = bf16[2048,768]{1,0:T(8,128)(2,1)} fusion(bf16[1024,768]{1,0:T(8,128)(2,1)S(1)} %bitcast.91, s32[2048]{0:T(1024)S(1)} %copy-done.9), kind=kCustom, calls=%fused_computation.7.clone | custom fusion | bytes 6299648 | tf_op jit(solution)/shard_map/jit(_take)/gather | solution.py:63
  234.0 3.3 %broadcast_select_fusion = bf16[2048,768]{1,0:T(8,128)(2,1)} fusion(bf16[2048,768]{1,0:T(8,128)(2,1)} %gather_fusion.10, pred[2048]{0:T(1024)(128)(4,1)S(1)} %copy-done.14), kind=kLoop, calls=%fused_computation.44 | loop fusion | flops 1572864 | bytes 6293504 | tf_op jit(solution)/shard_map/jit(_take)/select_n | solution.py:63
  237.3 4.9 %all-to-all-done.1 = bf16[32,64,768]{2,1,0:T(8,128)(2,1)} async-done(((bf16[32,64,768]{2,1,0:T(8,128)(2,1)}), bf16[32,64,768]{2,1,0:T(8,128)(2,1)}, u32[]{:S(2)}, u32[]{:S(2)}) %all-to-all-start.1) | async-done | bytes 3145760 | tf_op jit(solution)/shard_map/all_to_all | solution.py:92
  242.3 3.6 %all-to-all-start.3 = ((bf16[32,64,768]{2,1,0:T(8,128)(2,1)}), bf16[32,64,768]{2,1,0:T(8,128)(2,1)S(1)}, u32[]{:S(2)}, u32[]{:S(2)}) async-start(bf16[32,64,768]{2,1,0:T(8,128)(2,1)} %bitcast.95), calls=%async_computation.3 | async-start | bytes 6291456 | tf_op jit(solution)/shard_map/all_to_all | solution.py:92
  246.0 7.9 %gather_fusion.5 = bf16[1024,768]{1,0:T(8,128)(2,1)} fusion(bf16[2048,768]{1,0:T(8,128)(2,1)} %bitcast.19, s32[1024]{0:T(1024)S(1)} %broadcast_clamp_fusion.1), kind=kCustom, calls=%fused_computation.9.clone | custom fusion | bytes 3149824 | tf_op jit(solution)/shard_map/jit(_take)/gather | solution.py:68
  253.8 34.4 %all-to-all-done.3 = bf16[32,64,768]{2,1,0:T(8,128)(2,1)S(1)} async-done(((bf16[32,64,768]{2,1,0:T(8,128)(2,1)}), bf16[32,64,768]{2,1,0:T(8,128)(2,1)S(1)}, u32[]{:S(2)}, u32[]{:S(2)}) %all-to-all-start.3) | async-done | bytes 3145760 | tf_op jit(solution)/shard_map/all_to_all | solution.py:92
  288.2 1.7 copy-done.4
  289.9 8.0 %gather_fusion.11 = bf16[1024,768]{1,0:T(8,128)(2,1)} fusion(bf16[2048,768]{1,0:T(8,128)(2,1)} %bitcast.92, s32[1024]{0:T(1024)S(1)} %broadcast_clamp_fusion), kind=kCustom, calls=%fused_computation.11.clone | custom fusion | bytes 3149824 | tf_op jit(solution)/shard_map/jit(_take)/gather | solution.py:68
  297.9 1.8 add_convert_fusion.1
  300.3 1.8 add_convert_fusion
  (108 shorter events, 9.5 us)
Async XLA Ops:
  0.6 38.3 %copy-start.8 = (s32[1024,1]{0,1:T(1,128)S(1)}, s32[1024,1]{0,1:T(1,128)}, u32[]{:S(2)}) copy-start(s32[1024,1]{0,1:T(1,128)} %param.22) | copy-start | bytes 12292
  39.3 39.4 %copy-start.7 = (s32[1024,1]{0,1:T(1,128)S(1)}, s32[1024,1]{0,1:T(1,128)}, u32[]{:S(2)}) copy-start(s32[1024,1]{0,1:T(1,128)} %param.19) | copy-start | bytes 12292
  39.3 44.9 %copy-start = (bf16[1024,768]{1,0:T(8,128)(2,1)S(1)}, bf16[1024,768]{1,0:T(8,128)(2,1)}, u32[]{:S(2)}) copy-start(bf16[1024,768]{1,0:T(8,128)(2,1)} %param.18) | copy-start | bytes 4718596
  79.3 0.6 copy-start.10
  97.0 50.6 %all-to-all-start = ((bf16[32,64,768]{2,1,0:T(8,128)(2,1)}), bf16[32,64,768]{2,1,0:T(8,128)(2,1)}, u32[]{:S(2)}, u32[]{:S(2)}) async-start(bf16[32,64,768]{2,1,0:T(8,128)(2,1)} %bitcast.14), calls=%async_computation | async-start | bytes 6291456 | tf_op jit(solution)/shard_map/all_to_all | solution.py:86
  121.6 12.0 %copy-start.2 = (bf16[1024,768]{1,0:T(8,128)(2,1)S(1)}, bf16[1024,768]{1,0:T(8,128)(2,1)}, u32[]{:S(2)}) copy-start(bf16[1024,768]{1,0:T(8,128)(2,1)} %param.21) | copy-start | bytes 4718596
  129.2 13.8 %copy-start.12 = (s32[1024]{0:T(1024)}, s32[1024]{0:T(1024)S(1)}, u32[]{:S(2)}) copy-start(s32[1024]{0:T(1024)S(1)} %get-tuple-element.23) | copy-start | bytes 12292
  147.6 48.8 %all-to-all-start.2 = ((bf16[32,64,768]{2,1,0:T(8,128)(2,1)}), bf16[32,64,768]{2,1,0:T(8,128)(2,1)}, u32[]{:S(2)}, u32[]{:S(2)}) async-start(bf16[32,64,768]{2,1,0:T(8,128)(2,1)} %bitcast.35), calls=%async_computation.2 | async-start | bytes 6291456 | tf_op jit(solution)/shard_map/all_to_all | solution.py:86
  196.4 45.9 %all-to-all-start.1 = ((bf16[32,64,768]{2,1,0:T(8,128)(2,1)}), bf16[32,64,768]{2,1,0:T(8,128)(2,1)}, u32[]{:S(2)}, u32[]{:S(2)}) async-start(bf16[32,64,768]{2,1,0:T(8,128)(2,1)} %bitcast.18), calls=%async_computation.1 | async-start | bytes 6291456 | tf_op jit(solution)/shard_map/all_to_all | solution.py:92
  207.3 17.2 %copy-start.9 = (s32[2048]{0:T(1024)S(1)}, s32[2048]{0:T(1024)}, u32[]{:S(2)}) copy-start(s32[2048]{0:T(1024)} %fusion.47) | copy-start | bytes 24580
  224.5 9.5 %copy-start.14 = (pred[2048]{0:T(1024)(128)(4,1)S(1)}, pred[2048]{0:T(1024)(128)(4,1)}, u32[]{:S(2)}) copy-start(pred[2048]{0:T(1024)(128)(4,1)} %compare_and_fusion) | copy-start | bytes 6148
  242.3 3.6 %copy-start.11 = (s32[1024]{0:T(1024)S(1)}, s32[1024]{0:T(1024)}, u32[]{:S(2)}) copy-start(s32[1024]{0:T(1024)} %copy-done.10) | copy-start | bytes 12292
  242.3 3.7 %copy-start.13 = (s32[1024]{0:T(1024)S(1)}, s32[1024]{0:T(1024)}, u32[]{:S(2)}) copy-start(s32[1024]{0:T(1024)} %copy-done.12) | copy-start | bytes 12292
  242.3 45.9 %all-to-all-start.3 = ((bf16[32,64,768]{2,1,0:T(8,128)(2,1)}), bf16[32,64,768]{2,1,0:T(8,128)(2,1)S(1)}, u32[]{:S(2)}, u32[]{:S(2)}) async-start(bf16[32,64,768]{2,1,0:T(8,128)(2,1)} %bitcast.95), calls=%async_computation.3 | async-start | bytes 6291456 | tf_op jit(solution)/shard_map/all_to_all | solution.py:92
  288.2 1.7 copy-start.4
  289.8 8.0 %copy-start.1 = (bf16[1024,768]{1,0:T(8,128)(2,1)S(1)}, bf16[1024,768]{1,0:T(8,128)(2,1)}, u32[]{:S(2)}) copy-start(bf16[1024,768]{1,0:T(8,128)(2,1)} %param.18) | copy-start | bytes 4718596
  289.8 8.0 %copy-start.5 = (bf16[1024,768]{1,0:T(8,128)(2,1)S(1)}, bf16[1024,768]{1,0:T(8,128)(2,1)}, u32[]{:S(2)}) copy-start(bf16[1024,768]{1,0:T(8,128)(2,1)} %gather_fusion.5) | copy-start | bytes 4718596
  289.8 8.0 %copy-start.15 = (pred[1024]{0:T(1024)(128)(4,1)S(1)}, pred[1024]{0:T(1024)(128)(4,1)}, u32[]{:S(2)}) copy-start(pred[1024]{0:T(1024)(128)(4,1)} %get-tuple-element.24) | copy-start | bytes 3076
  289.8 8.1 %copy-start.17 = (f32[1024,1]{0,1:T(1,128)S(1)}, f32[1024,1]{0,1:T(1,128)}, u32[]{:S(2)}) copy-start(f32[1024,1]{0,1:T(1,128)} %param.20) | copy-start | bytes 12292
  297.9 1.8 copy-start.3
  297.9 2.4 copy-start.6
  297.9 2.4 copy-start.16
  297.9 2.4 copy-start.18
where the time goes:
time: 303 us; the launch traced here: 302 us
  local copies, waits for them, and re-layouts  112 us (37%)
  blocking collectives  67.5 us (22%)
  waiting for transfers between devices  44.5 us (15%)
  matrix products  34.4 us (11%)
  other arithmetic  23 us (8%)
  starting transfers between devices  19.6 us (6%)
    all_gather x2, blocking collectives, moe_micro(): all_counts = lax.all_gather(counts, 'expert')  67.5 us
    all_to_all x2, waiting for transfers between devices, moe_micro(): returned = lax.all_to_all(back_rows, 'expert', 0, 0, tiled=True)  39.3 us
    dot_general x2, matrix products, expert_ffn(): jnp.einsum('ecf,efd->ecd', hidden, w_down, preferred_element_type=jnp.flo...  34.4 us
    gather x2, local copies, waits for them, and re-layouts, dispatch_rows(): jnp.take(tok_rows, slot_token, axis=0, mode='fill', fill_value=0)  18.9 us
    gather x2, local copies, waits for them, and re-layouts, expand_rows(): jnp.take(expert_out.reshape(local_experts * capacity, model_dim), src_ind...  18.9 us
    gather x4, local copies, waits for them, and re-layouts, compact_rows(): source_first = jnp.take_along_axis(first_mine.T, source_safe, axis=1)  18.1 us
    gather x2, local copies, waits for them, and re-layouts, combine_rows(): jnp.take(returned, send_pos, axis=0, mode='fill', fill_value=0)  15.9 us
    gather x2, local copies, waits for them, and re-layouts, compact_rows(): jnp.take(recv_rows, row_index.reshape(-1), axis=0, mode='fill', fill_valu...  13.5 us
  transfers between devices with their start and end apart: 4, of which 3 were waited for; matrix products, arithmetic and copies ran while one was open for 42% of the time, Pallas kernels for 0%

commit v1 on v0

v1 whole, which is shorter than its diff:
```python
import functools

import jax
import jax.numpy as jnp
from jax import lax
from jax.experimental import pallas as pl
from jax.experimental.pallas import tpu as pltpu
from jax.sharding import PartitionSpec as P

BF16 = jnp.bfloat16
F32 = jnp.float32
LANES = 128


def iota(shape, dim):
    return lax.broadcasted_iota(jnp.int32, shape, dim)


def one_hot(mask):
    return jnp.where(mask, 1.0, 0.0).astype(BF16)


def dot(a, b):
    return jnp.dot(a, b, preferred_element_type=F32)


def dot_nt(a, b):
    return lax.dot_general(a, b, (((1,), (1,)), ((), ())), preferred_element_type=F32)


def to_column(row):
    return jnp.transpose(jnp.broadcast_to(row, (LANES, row.shape[1])))


def lane_match(column, width, base):
    lane = iota(column.shape, 1)
    parts = [one_hot(column == lane + (base + k * LANES)) for k in range(width // LANES)]
    return jnp.concatenate(parts, axis=1)


def kernel(group, stride, ids_a, gate_a, ids_b, gate_b, x_a, x_b, w_up, w_down, y_a, y_b,
           x_v, send, recv, back, counts, table, w1, w2, hidden, rows_in, acc, y_v,
           posc, slotr, slotc,
           x_sem, y_sem, w_sem, count_sems, send_sems, recv_sems, ret_sems, back_sems):
    me = lax.axis_index('expert')
    local, _, load, dim = send.shape[1:]
    n_tok = x_v.shape[1]
    n_exp = local * group
    span = group * load
    cap = rows_in.shape[0]
    ffn = hidden.shape[1]
    ids_refs, gate_refs = (ids_a, ids_b), (gate_a, gate_b)
    x_refs, y_refs = (x_a, x_b), (y_a, y_b)

    def peer(i):
        return lax.rem(me + i * stride, group)

    barrier = pltpu.get_barrier_semaphore()

    @pl.loop(1, group)
    def _(i):
        pl.semaphore_signal(barrier, inc=1, device_id={'expert': peer(i)}, device_id_type=pl.DeviceIdType.MESH)

    def x_copy(m):
        return pltpu.make_async_copy(x_refs[m], x_v.at[m], x_sem.at[m])

    def y_copy(m):
        return pltpu.make_async_copy(y_v.at[m], y_refs[m], y_sem.at[m])

    def w_copies(e, slot):
        return (pltpu.make_async_copy(w_up.at[e], w1.at[slot], w_sem.at[slot, 0]),
                pltpu.make_async_copy(w_down.at[e], w2.at[slot], w_sem.at[slot, 1]))

    x_copy(0).start()
    x_copy(1).start()
    for e in range(2):
        for copy in w_copies(e, e):
            copy.start()

    upper = one_hot(iota((n_tok, n_tok), 0) < iota((n_tok, n_tok), 1))
    pos_rows, count_rows = [], []
    for m in range(2):
        ids = ids_refs[m][...]
        hot = one_hot(iota((n_exp, n_tok), 0) == ids)
        earlier = dot(hot, upper)
        rank = jnp.sum(hot.astype(F32) * earlier, axis=0, keepdims=True).astype(jnp.int32)
        count_rows.append(dot_nt(jnp.ones((8, n_tok), BF16), hot))
        pos = lax.rem(ids, local) * span + lax.div(ids, local) * load + rank
        pos_rows.append(pos)
        posc[m] = to_column(pos)
    counts[...] = jnp.where(iota((8, n_exp), 0) < 4, count_rows[0], count_rows[1])

    def gather_rows(m):
        x_copy(m).wait()

        @pl.loop(0, local)
        def _(e):
            pick = one_hot(iota((span, n_tok), 0) == pos_rows[m] - e * span)
            send[m, e] = dot(pick, x_v[m]).astype(BF16).reshape(group, load, dim)

    def dispatch(m):
        pltpu.make_async_copy(send.at[m, :, me], recv.at[m, :, me], recv_sems.at[m]).start()

        @pl.loop(1, group)
        def _(i):
            pltpu.make_async_remote_copy(
                src_ref=send.at[m, :, peer(i)], dst_ref=recv.at[m, :, me],
                send_sem=send_sems.at[m], recv_sem=recv_sems.at[m],
                device_id={'expert': peer(i)}, device_id_type=pl.DeviceIdType.MESH).start()

    def give_back(m, e):
        pltpu.make_async_copy(recv.at[m, e, me], back.at[m, e, me], back_sems.at[m, e]).start()

        @pl.loop(1, group)
        def _(i):
            pltpu.make_async_remote_copy(
                src_ref=recv.at[m, e, peer(i)], dst_ref=back.at[m, e, me],
                send_sem=ret_sems.at[m], recv_sem=back_sems.at[m, e],
                device_id={'expert': peer(i)}, device_id_type=pl.DeviceIdType.MESH).start()

    gather_rows(0)
    pl.semaphore_wait(barrier, group - 1)

    pltpu.make_async_copy(counts, table.at[me], count_sems.at[1]).start()

    @pl.loop(1, group)
    def _(i):
        pltpu.make_async_remote_copy(
            src_ref=counts, dst_ref=table.at[me],
            send_sem=count_sems.at[0], recv_sem=count_sems.at[1],
            device_id={'expert': peer(i)}, device_id_type=pl.DeviceIdType.MESH).start()

    dispatch(0)
    gather_rows(1)
    dispatch(1)

    pltpu.make_async_copy(table, table, count_sems.at[1]).wait()
    lower = one_hot(iota((group, group), 1) <= iota((group, group), 0))
    mine = one_hot(iota((8, n_exp), 1) - me * local == iota((8, n_exp), 0))
    mine = jnp.where(iota((8, n_exp), 0) < local, mine.astype(F32), 0.0).astype(BF16)
    spread = one_hot(lax.div(iota((group, span), 1), load) == iota((group, span), 0))
    row_in_load = lax.rem(iota((8, span), 1), load)
    for m in range(2):
        cnt = table[:, 4 * m, :]
        inclusive = dot(lower, cnt.astype(BF16))
        first = jnp.minimum(inclusive - cnt, float(cap))
        kept = jnp.minimum(inclusive, float(cap)) - first
        first_row = dot(dot_nt(mine, first.astype(BF16)).astype(BF16), spread).astype(jnp.int32)
        kept_row = dot(dot_nt(mine, kept.astype(BF16)).astype(BF16), spread).astype(jnp.int32)
        slot = jnp.where(row_in_load < kept_row, first_row + row_in_load, -1)
        for e in range(local):
            row = slot[e:e + 1]
            slotr[m, e] = jnp.broadcast_to(row, (8, span))
            slotc[m, e] = to_column(row)

    tile = min(512, ffn)

    def experts(m):
        pltpu.make_async_copy(recv.at[m], recv.at[m], recv_sems.at[m]).wait()

        @pl.loop(0, local)
        def _(e):
            step = m * local + e
            slot = lax.rem(step, 2)
            pick = one_hot(iota((cap, span), 0) == slotr[m, e, 0:1])
            rows_in[...] = dot(pick, recv[m, e].reshape(span, dim)).astype(BF16)
            for copy in w_copies(e, slot):
                copy.wait()

            @pl.loop(0, ffn // tile)
            def _(f):
                cols = pl.ds(pl.multiple_of(f * tile, tile), tile)
                hidden[:, cols] = jax.nn.gelu(dot(rows_in[...], w1[slot, :, cols])).astype(BF16)

            out = dot(hidden[...], w2[slot]).astype(BF16)
            place = lane_match(slotc[m, e], cap, 0)
            recv[m, e] = dot(place, out).astype(BF16).reshape(group, load, dim)
            give_back(m, e)

            @pl.when(step + 2 < 2 * local)
            def _():
                for copy in w_copies(lax.rem(e + 2, local), slot):
                    copy.start()

    experts(0)
    experts(1)

    rows = min(256, n_tok)

    def combine(m):
        for e in range(local):
            pltpu.make_async_copy(back.at[m, e], back.at[m, e], back_sems.at[m, e]).wait()

            @pl.loop(0, n_tok // rows)
            def _(b):
                part = pl.ds(pl.multiple_of(b * rows, rows), rows)
                take = lane_match(posc[m, part], span, e * span)
                got = dot(take, back[m, e].reshape(span, dim))
                if e > 0:
                    got = got + acc[part]
                acc[part] = got

        gate_col = to_column(gate_refs[m][...])
        for k in range(dim // LANES):
            cols = slice(k * LANES, (k + 1) * LANES)
            y_v[m, :, cols] = (x_v[m, :, cols].astype(F32) + gate_col * acc[:, cols]).astype(BF16)
        y_copy(m).start()

    combine(0)
    combine(1)

    pltpu.make_async_copy(table.at[0:group - 1], table.at[0:group - 1], count_sems.at[0]).wait()
    for m in range(2):
        sent = send.at[m, :, 0:group - 1]
        pltpu.make_async_copy(sent, sent, send_sems.at[m]).wait()
        pltpu.make_async_copy(sent, sent, ret_sems.at[m]).wait()
        y_copy(m).wait()


def moe(group, x_a, idx_a, gate_a, x_b, idx_b, gate_b, w_up, w_down):
    n_tok, dim = x_a.shape
    local, _, ffn = w_up.shape
    n_exp = local * group
    load = 2 * n_tok // n_exp
    cap = n_tok // local
    span = group * load
    rows = [a.reshape(1, n_tok) for a in (idx_a, gate_a, idx_b, gate_b)]
    vmem, hbm = pl.BlockSpec(memory_space=pltpu.VMEM), pl.BlockSpec(memory_space=pl.ANY)
    dma = pltpu.SemaphoreType.DMA
    exchange = (2, local, group, load, dim)
    return pl.pallas_call(
        functools.partial(kernel, group, 11),
        out_shape=(jax.ShapeDtypeStruct((n_tok, dim), BF16),) * 2,
        in_specs=[vmem] * 4 + [hbm] * 4,
        out_specs=(hbm, hbm),
        scratch_shapes=[
            pltpu.VMEM((2, n_tok, dim), BF16),
            pltpu.VMEM(exchange, BF16),
            pltpu.VMEM(exchange, BF16),
            pltpu.VMEM(exchange, BF16),
            pltpu.VMEM((8, n_exp), F32),
            pltpu.VMEM((group, 8, n_exp), F32),
            pltpu.VMEM((2, dim, ffn), BF16),
            pltpu.VMEM((2, ffn, dim), BF16),
            pltpu.VMEM((cap, ffn), BF16),
            pltpu.VMEM((cap, dim), BF16),
            pltpu.VMEM((n_tok, dim), F32),
            pltpu.VMEM((2, n_tok, dim), BF16),
            pltpu.VMEM((2, n_tok, LANES), jnp.int32),
            pltpu.VMEM((2, local, 8, span), jnp.int32),
            pltpu.VMEM((2, local, span, LANES), jnp.int32),
            dma((2,)), dma((2,)), dma((2, 2)), dma((2,)), dma((2,)), dma((2,)), dma((2,)), dma((2, local)),
        ],
        compiler_params=pltpu.CompilerParams(
            collective_id=0, has_side_effects=True, vmem_limit_bytes=64 * 1024 * 1024 - 65536),
        name='moe',
    )(*rows, x_a, x_b, w_up, w_down)


def solution(mesh):
    row_spec = P(('data', 'expert'), None)
    weight_spec = P('expert', None, None)
    return jax.shard_map(
        functools.partial(moe, mesh.shape['expert']), mesh=mesh,
        in_specs=(row_spec,) * 6 + (weight_spec,) * 2, out_specs=(row_spec, row_spec), check_vma=False)
```

time: 303 us -> 177 us (0.58)
  the two profiles are of different devices: /device:TPU:98 before, /device:TPU:110 now
where the time goes in v1:
time: 177 us
  Pallas kernels  172 us (97%)
  local copies, waits for them, and re-layouts  3.92 us (2%)
    pallas_call x1, Pallas kernels, moe(): pl.pallas_call(functools.partial(kernel, group, 11), out_shape=(jax.Shape...  172 us
    unnamed x4, local copies, waits for them, and re-layouts  3.92 us

profile of v1, /device:TPU:110, one launch (start us, length us, event | category | flops | bytes accessed | tf_op | source)
XLA Modules:
  0.0 176.5 jit_solution(3225620872461874017)
XLA Ops:
  0.6 172.0 %moe.1 = (bf16[1024,768]{1,0:T(8,128)(2,1)}, bf16[1024,768]{1,0:T(8,128)(2,1)}) custom-call(s32[1,1024]{1,0:T(1,128)} %bitcast.4, f32[1,1024]{1,0:T(1,128)} %bitcast.5, s32[1,1024]{1,0:T(1,128)} %bitcast.6, f32[1,1024]{1,0:T(1,128)} %bitcast.7, bf16[1024,768]{1,0:T(8,128)(2,1)} %x_a.1, bf16[1024,768]{1,0:T(8,128)(2,1)} %x_b.1, bf16[4,768,3072]{2,1,0:T(8,128)(2,1)} %w_up.1, ...), custom_call_target="tpu_custom_call" | custom-call | tf_op jit(solution)/shard_map/moe/pallas_call | solution.py:231
  172.6 0.0 copy-start
  172.6 2.8 %copy.12 = bf16[1024,768]{1,0:T(8,128)(2,1)} copy(bf16[1024,768]{1,0:T(8,128)(2,1)} %get-tuple-element.4) | data formatting | bytes 3145728
  175.4 0.0 copy-done
  175.4 1.1 copy.13
Async XLA Ops:
  172.6 2.8 %copy-start = (bf16[1024,768]{1,0:T(8,128)(2,1)S(1)}, bf16[1024,768]{1,0:T(8,128)(2,1)}, u32[]{:S(2)}) copy-start(bf16[1024,768]{1,0:T(8,128)(2,1)} %get-tuple-element.5) | copy-start | bytes 4718596

commit v2 on v1

--- a/solution.py
+++ b/solution.py
@@ -1,4 +1,5 @@
 import functools
+import math
 
 import jax
 import jax.numpy as jnp
@@ -38,9 +39,22 @@
     return jnp.concatenate(parts, axis=1)
 
 
-def kernel(group, stride, ids_a, gate_a, ids_b, gate_b, x_a, x_b, w_up, w_down, y_a, y_b,
+def displacements(side):
+    turns = list(range(1, side)) + [0]
+    back = [(side - d) % side for d in turns]
+    ahead = range(1, (side + 1) // 2)
+    queues = [[(dx, d) for dx in ahead for d in turns],
+              [(side - dx, d) for dx in ahead for d in back],
+              [(side // 2, d) for d in turns] if side % 2 == 0 else [],
+              [(0, d) for d in turns if d]]
+    steps = max(len(q) for q in queues)
+    order = [q[i] for i in range(steps) for q in queues if i < len(q)]
+    return [(dx, dy, flip) for dx, dy in order for flip in (0, 1)] + [(0, 0, 1)]
+
+
+def kernel(group, ids_a, gate_a, ids_b, gate_b, x_a, x_b, w_up, w_down, y_a, y_b,
            x_v, send, recv, back, counts, table, w1, w2, hidden, rows_in, acc, y_v,
-           posc, slotr, slotc,
+           posc, gatec, slotr, slotc, takes,
            x_sem, y_sem, w_sem, count_sems, send_sems, recv_sems, ret_sems, back_sems):
     me = lax.axis_index('expert')
     local, _, load, dim = send.shape[1:]
@@ -52,8 +66,18 @@
     ids_refs, gate_refs = (ids_a, ids_b), (gate_a, gate_b)
     x_refs, y_refs = (x_a, x_b), (y_a, y_b)
 
+    side = math.isqrt(group // 2)
+    core = lax.rem(me, 2)
+    my_x, my_y = lax.rem(lax.div(me, 2), side), lax.div(me, 2 * side)
+    hops = displacements(side)
+
+    def towards(dx, dy, flip):
+        x = lax.rem(my_x + dx + core * (side - 2 * dx), side)
+        y = lax.rem(my_y + dy + core * (side - 2 * dy), side)
+        return (y * side + x) * 2 + lax.rem(core + flip, 2)
+
     def peer(i):
-        return lax.rem(me + i * stride, group)
+        return lax.rem(me + i, group)
 
     barrier = pltpu.get_barrier_semaphore()
 
@@ -63,9 +87,6 @@
 
     def x_copy(m):
         return pltpu.make_async_copy(x_refs[m], x_v.at[m], x_sem.at[m])
-
-    def y_copy(m):
-        return pltpu.make_async_copy(y_v.at[m], y_refs[m], y_sem.at[m])
 
     def w_copies(e, slot):
         return (pltpu.make_async_copy(w_up.at[e], w1.at[slot], w_sem.at[slot, 0]),
@@ -77,62 +98,66 @@
         for copy in w_copies(e, e):
             copy.start()
 
-    upper = one_hot(iota((n_tok, n_tok), 0) < iota((n_tok, n_tok), 1))
-    pos_rows, count_rows = [], []
-    for m in range(2):
+    before = one_hot(iota((LANES, LANES), 0) < iota((LANES, LANES), 1))
+    ones = jnp.ones((8, n_tok), BF16)
+
+    def positions(m):
         ids = ids_refs[m][...]
         hot = one_hot(iota((n_exp, n_tok), 0) == ids)
-        earlier = dot(hot, upper)
-        rank = jnp.sum(hot.astype(F32) * earlier, axis=0, keepdims=True).astype(jnp.int32)
-        count_rows.append(dot_nt(jnp.ones((8, n_tok), BF16), hot))
+        seen = jnp.zeros((n_exp, 1), F32)
+        ranks = []
+        for k in range(n_tok // LANES):
+            block = hot[:, k * LANES:(k + 1) * LANES]
+            wide = block.astype(F32)
+            ranks.append(jnp.sum(wide * (dot(block, before) + seen), axis=0, keepdims=True))
+            seen = seen + jnp.sum(wide, axis=1, keepdims=True)
+        rank = jnp.concatenate(ranks, axis=1).astype(jnp.int32)
         pos = lax.rem(ids, local) * span + lax.div(ids, local) * load + rank
-        pos_rows.append(pos)
-        posc[m] = to_column(pos)
-    counts[...] = jnp.where(iota((8, n_exp), 0) < 4, count_rows[0], count_rows[1])
-
-    def gather_rows(m):
+        return pos, hot
+
+    def gather_rows(m, pos):
         x_copy(m).wait()
 
         @pl.loop(0, local)
         def _(e):
-            pick = one_hot(iota((span, n_tok), 0) == pos_rows[m] - e * span)
+            pick = one_hot(iota((span, n_tok), 0) == pos - e * span)
             send[m, e] = dot(pick, x_v[m]).astype(BF16).reshape(group, load, dim)
 
-    def dispatch(m):
-        pltpu.make_async_copy(send.at[m, :, me], recv.at[m, :, me], recv_sems.at[m]).start()
-
-        @pl.loop(1, group)
-        def _(i):
-            pltpu.make_async_remote_copy(
-                src_ref=send.at[m, :, peer(i)], dst_ref=recv.at[m, :, me],
-                send_sem=send_sems.at[m], recv_sem=recv_sems.at[m],
-                device_id={'expert': peer(i)}, device_id_type=pl.DeviceIdType.MESH).start()
+    def push(src, dst, send_sem, recv_sem, to):
+        pltpu.make_async_remote_copy(
+            src_ref=src, dst_ref=dst, send_sem=send_sem, recv_sem=recv_sem,
+            device_id={'expert': to}, device_id_type=pl.DeviceIdType.MESH).start()
+
+    def dispatch(m, part):
+        pltpu.make_async_copy(send.at[m, part, me], recv.at[m, part, me], recv_sems.at[m]).start()
+        for hop in hops:
+            to = towards(*hop)
+            push(send.at[m, part, to], recv.at[m, part, me], send_sems.at[m], recv_sems.at[m], to)
 
     def give_back(m, e):
         pltpu.make_async_copy(recv.at[m, e, me], back.at[m, e, me], back_sems.at[m, e]).start()
-
-        @pl.loop(1, group)
-        def _(i):
-            pltpu.make_async_remote_copy(
-                src_ref=recv.at[m, e, peer(i)], dst_ref=back.at[m, e, me],
-                send_sem=ret_sems.at[m], recv_sem=back_sems.at[m, e],
-                device_id={'expert': peer(i)}, device_id_type=pl.DeviceIdType.MESH).start()
-
-    gather_rows(0)
+        for hop in hops:
+            to = towards(*hop)
+            push(recv.at[m, e, to], back.at[m, e, me], ret_sems.at[m], back_sems.at[m, e], to)
+
+    half = local // 2
+    pos_a, hot_a = positions(0)
+    gather_rows(0, pos_a)
     pl.semaphore_wait(barrier, group - 1)
-
+    dispatch(0, slice(0, local))
+    pos_b, hot_b = positions(1)
+    gather_rows(1, pos_b)
+    dispatch(1, slice(0, half))
+
+    counts[...] = jnp.where(iota((8, n_exp), 0) < 4, dot_nt(ones, hot_a), dot_nt(ones, hot_b))
+    for m, pos in enumerate((pos_a, pos_b)):
+        posc[m] = to_column(pos)
+        gatec[m] = to_column(gate_refs[m][...])
     pltpu.make_async_copy(counts, table.at[me], count_sems.at[1]).start()
 
     @pl.loop(1, group)
     def _(i):
-        pltpu.make_async_remote_copy(
-            src_ref=counts, dst_ref=table.at[me],
-            send_sem=count_sems.at[0], recv_sem=count_sems.at[1],
-            device_id={'expert': peer(i)}, device_id_type=pl.DeviceIdType.MESH).start()
-
-    dispatch(0)
-    gather_rows(1)
-    dispatch(1)
+        push(counts, table.at[me], count_sems.at[0], count_sems.at[1], peer(i))
 
     pltpu.make_async_copy(table, table, count_sems.at[1]).wait()
     lower = one_hot(iota((group, group), 1) <= iota((group, group), 0))
@@ -157,6 +182,8 @@
 
     def experts(m):
         pltpu.make_async_copy(recv.at[m], recv.at[m], recv_sems.at[m]).wait()
+        if m == 0:
+            dispatch(1, slice(half, local))
 
         @pl.loop(0, local)
         def _(e):
@@ -186,25 +213,30 @@
     experts(1)
 
     rows = min(256, n_tok)
+    last = local - 1
 
     def combine(m):
+        @pl.loop(0, n_tok // rows)
+        def _(b):
+            part = pl.ds(pl.multiple_of(b * rows, rows), rows)
+            takes[part] = lane_match(posc[m, part], span, last * span)
+
         for e in range(local):
             pltpu.make_async_copy(back.at[m, e], back.at[m, e], back_sems.at[m, e]).wait()
 
             @pl.loop(0, n_tok // rows)
             def _(b):
                 part = pl.ds(pl.multiple_of(b * rows, rows), rows)
-                take = lane_match(posc[m, part], span, e * span)
+                take = takes[part] if e == last else lane_match(posc[m, part], span, e * span)
                 got = dot(take, back[m, e].reshape(span, dim))
                 if e > 0:
                     got = got + acc[part]
-                acc[part] = got
-
-        gate_col = to_column(gate_refs[m][...])
-        for k in range(dim // LANES):
-            cols = slice(k * LANES, (k + 1) * LANES)
-            y_v[m, :, cols] = (x_v[m, :, cols].astype(F32) + gate_col * acc[:, cols]).astype(BF16)
-        y_copy(m).start()
+                if e < last:
+                    acc[part] = got
+                else:
+                    gate = jnp.concatenate([gatec[m, part]] * (dim // LANES), axis=1)
+                    y_v[m, part] = (x_v[m, part].astype(F32) + gate * got).astype(BF16)
+                    pltpu.make_async_copy(y_v.at[m, part], y_refs[m].at[part], y_sem.at[m]).start()
 
     combine(0)
     combine(1)
@@ -214,7 +246,7 @@
         sent = send.at[m, :, 0:group - 1]
         pltpu.make_async_copy(sent, sent, send_sems.at[m]).wait()
         pltpu.make_async_copy(sent, sent, ret_sems.at[m]).wait()
-        y_copy(m).wait()
+        pltpu.make_async_copy(y_v.at[m], y_refs[m], y_sem.at[m]).wait()
 
 
 def moe(group, x_a, idx_a, gate_a, x_b, idx_b, gate_b, w_up, w_down):
@@ -229,7 +261,7 @@
     dma = pltpu.SemaphoreType.DMA
     exchange = (2, local, group, load, dim)
     return pl.pallas_call(
-        functools.partial(kernel, group, 11),
+        functools.partial(kernel, group),
         out_shape=(jax.ShapeDtypeStruct((n_tok, dim), BF16),) * 2,
         in_specs=[vmem] * 4 + [hbm] * 4,
         out_specs=(hbm, hbm),
@@ -247,8 +279,10 @@
             pltpu.VMEM((n_tok, dim), F32),
             pltpu.VMEM((2, n_tok, dim), BF16),
             pltpu.VMEM((2, n_tok, LANES), jnp.int32),
+            pltpu.VMEM((2, n_tok, LANES), F32),
             pltpu.VMEM((2, local, 8, span), jnp.int32),
             pltpu.VMEM((2, local, span, LANES), jnp.int32),
+            pltpu.VMEM((n_tok, span), BF16),
             dma((2,)), dma((2,)), dma((2, 2)), dma((2,)), dma((2,)), dma((2,)), dma((2,)), dma((2, local)),
         ],
         compiler_params=pltpu.CompilerParams(

time: 177 us -> 185 us (1.045)
  the two profiles are of different devices: /device:TPU:110 before, /device:TPU:97 now
where the time goes in v2:
time: 185 us
  Pallas kernels  180 us (97%)
  local copies, waits for them, and re-layouts  3.92 us (2%)
    pallas_call x1, Pallas kernels, moe(): pl.pallas_call(functools.partial(kernel, group), out_shape=(jax.ShapeDtyp...  180 us
    unnamed x4, local copies, waits for them, and re-layouts  3.92 us

profile of v2, /device:TPU:97, one launch (start us, length us, event | category | flops | bytes accessed | tf_op | source)
XLA Modules:
  0.0 185.0 jit_solution(8667508599406535772)
XLA Ops:
  0.6 180.4 %moe.1 = (bf16[1024,768]{1,0:T(8,128)(2,1)}, bf16[1024,768]{1,0:T(8,128)(2,1)}) custom-call(s32[1,1024]{1,0:T(1,128)} %bitcast.4, f32[1,1024]{1,0:T(1,128)} %bitcast.5, s32[1,1024]{1,0:T(1,128)} %bitcast.6, f32[1,1024]{1,0:T(1,128)} %bitcast.7, bf16[1024,768]{1,0:T(8,128)(2,1)} %x_a.1, bf16[1024,768]{1,0:T(8,128)(2,1)} %x_b.1, bf16[4,768,3072]{2,1,0:T(8,128)(2,1)} %w_up.1, ...), custom_call_target="tpu_custom_call" | custom-call | tf_op jit(solution)/shard_map/moe/pallas_call | solution.py:263
  181.1 0.0 copy-start
  181.1 2.8 %copy.12 = bf16[1024,768]{1,0:T(8,128)(2,1)} copy(bf16[1024,768]{1,0:T(8,128)(2,1)} %get-tuple-element.4) | data formatting | bytes 3145728
  183.9 0.0 copy-done
  183.9 1.1 copy.13
Async XLA Ops:
  181.1 2.8 %copy-start = (bf16[1024,768]{1,0:T(8,128)(2,1)S(1)}, bf16[1024,768]{1,0:T(8,128)(2,1)}, u32[]{:S(2)}) copy-start(bf16[1024,768]{1,0:T(8,128)(2,1)} %get-tuple-element.5) | copy-start | bytes 4718596
